TPU v7x, 32 devices: a whole 2x2x4 slice. The times are simulated.
32 devices in a mesh: replica: 4 (over y, x), fsdp: 8 (over z, core).
Axes of the slice: x: 2, y: 2, z: 4, core: 2. Of those that a mesh axis runs over, the one named last changes fastest.
Arguments:
- codes: int32 [4, 8192, 4096], P('replica', None, 'fsdp'), may hold values from -127 to 127
- scales: float32 [4, 32, 8192], P('replica', 'fsdp'), may hold values from 0.002 to 0.03
- master: float32 [8192, 4096], P(('replica', 'fsdp')), may hold values from -6 to 6
- momentum: float32 [8192, 4096], P(('replica', 'fsdp')), may hold values from -6 to 6
Outputs:
- new_master: float32 [8192, 4096], P(('replica', 'fsdp'))
- new_momentum: float32 [8192, 4096], P(('replica', 'fsdp'))
- weights: bfloat16 [8192, 4096], P(None, 'fsdp')
All inputs are finite; a program needn't handle non-finite values.
Results may differ from a plain program's by a relative error of at most 0.0075.
Values may be sent and summed in bfloat16 or wider, within the bound.
A program may use at most 128 MiB of HBM per device.

v0:
```python
import functools

import jax
import jax.numpy as jnp
from jax import lax
from jax.experimental import pallas as pl
from jax.experimental.pallas import tpu as pltpu
from jax.sharding import PartitionSpec as P

MESH = pl.DeviceIdType.MESH

outer_rate = 0.7
momentum_factor = 0.9

LAGS = (0, 2, 4, 6, 8, 10, 12)
RS1, RS2, X1, X2, AG1, AG2 = range(6)


def kernel(cfg, codes, scales, master, momentum, new_master, new_momentum, weights,
           delta, rs1e, rs1o, rs2e, rs2o, part, got, wsend, mast, mom, cbuf, flat, sbuf,
           send_sem, recv_sem, in_sem, state_sem, out_sem, own_sem):
    A, B, F, K, sub, width, blocks = cfg
    R, FS, block = A * B, F * sub, width // blocks
    r, f = lax.axis_index("replica"), lax.axis_index("fsdp")
    a, b = r // B, lax.rem(r, B)

    def a_peer(i):
        return lax.rem(a + 1 + i, A)

    def b_peer(i):
        return lax.rem(b + 1 + i, B)

    def f_peer(i):
        return lax.rem(f + 1 + i, F)

    def load(k):
        slot = lax.rem(k, 2)
        return (pltpu.make_async_copy(codes.at[:, k], cbuf.at[slot], in_sem.at[slot]),)

    scales_in = pltpu.make_async_copy(scales.at[0], flat.at[pl.ds(0, blocks)], state_sem.at[2])
    scales_in.start()
    for k in range(min(2, K)):
        for copy in load(k):
            copy.start()
    state_in = (
        pltpu.make_async_copy(master, mast, state_sem.at[0]),
        pltpu.make_async_copy(momentum, mom, state_sem.at[1]),
    )
    for copy in state_in:
        copy.start()

    barrier = pltpu.get_barrier_semaphore()
    for i in range(A - 1):
        pl.semaphore_signal(barrier, inc=1, device_id=(a_peer(i) * B + b, f), device_id_type=MESH)
    for i in range(B - 1):
        pl.semaphore_signal(barrier, inc=1, device_id=(a * B + b_peer(i), f), device_id_type=MESH)
    for i in range(F - 1):
        pl.semaphore_signal(barrier, inc=1, device_id=(r, f_peer(i)), device_id_type=MESH)
    scales_in.wait()

    def turn(i, carry):
        tile = flat[:, pl.ds(pl.multiple_of(i * 128, 128), 128)]
        sbuf[pl.ds(pl.multiple_of(i * 128, 128), 128), :] = jnp.transpose(tile)
        return carry

    lax.fori_loop(0, flat.shape[1] // 128, turn, 0, unroll=8)
    pl.semaphore_wait(barrier, A + B + F - 3)

    def send(stage, k, src, dst, device):
        pltpu.make_async_remote_copy(
            src_ref=src, dst_ref=dst, send_sem=send_sem.at[stage, k], recv_sem=recv_sem.at[stage, k],
            device_id=device, device_id_type=MESH,
        ).start()

    def wait_bytes(sem, stage, k, ref):
        pltpu.make_async_copy(ref, ref, sem.at[stage, k]).wait()

    def rows(j):
        return pl.ds(pl.multiple_of(j * sub, sub), sub)

    def f32(x):
        return x.astype(jnp.float32)

    def amount(stage, k, even):
        if stage == RS1:
            return rs1e.at[k // 2] if even else rs1o.at[k // 2]
        if stage == RS2:
            return rs2e.at[k // 2] if even else rs2o.at[k // 2]
        if stage in (X1, X2):
            return part.at[k, pl.ds(0, (F - 1) * sub)]
        first, second = (B - 1, B * (A - 1)) if even else (A - 1, A * (B - 1))
        count = first if stage == AG1 else second
        return delta.at[k, pl.ds(0, count)]

    def by_parity(k, fn):
        @pl.when(lax.rem(k, 2) == 0)
        def _():
            fn(True)

        if K > 1:
            @pl.when(lax.rem(k, 2) == 1)
            def _():
                fn(False)

    def stage0(k):
        slot = lax.rem(k, 2)
        for copy in load(k):
            copy.wait()

        def one(g, carry):
            q, j = g // F, lax.rem(g, F)
            for n in range(blocks):
                cols = pl.ds(n * block, block)
                value = f32(cbuf[slot, g, :, cols]) * sbuf[pl.ds(pl.multiple_of((g * K + k) * sub, sub), sub), pl.ds(n, 1)]
                delta[k, q, rows(j), cols] = value.astype(jnp.bfloat16)
            return carry

        lax.fori_loop(0, R * F, one, 0, unroll=4)

        @pl.when(k + 2 < K)
        def _():
            for copy in load(k + 2):
                copy.start()

        def go(even):
            if even:
                for i in range(B - 1):
                    bb = b_peer(i)
                    for aa in range(A):
                        send(RS1, k, delta.at[k, aa * B + bb], rs1e.at[k // 2, B - 2 - i, aa], (a * B + bb, f))
            else:
                for i in range(A - 1):
                    aa = a_peer(i)
                    send(RS1, k, delta.at[k, pl.ds(aa * B, B)], rs1o.at[k // 2, A - 2 - i], (aa * B + b, f))

        by_parity(k, go)

    def stage1(k):
        def go(even):
            wait_bytes(recv_sem, RS1, k, amount(RS1, k, even))
            buf, count, peers = (rs1e, B - 1, A - 1) if even else (rs1o, A - 1, B - 1)
            for i in range(peers):
                q = a_peer(i) if even else b_peer(i)
                target = q * B + b if even else a * B + q

                def add(j, carry):
                    total = f32(delta[k, target, rows(j), :])
                    for s in range(count):
                        total = total + f32(buf[k // 2, s, q, rows(j), :])
                    buf[k // 2, 0, q, rows(j), :] = total.astype(jnp.bfloat16)
                    return carry

                lax.fori_loop(0, F, add, 0, unroll=4)
                dst = rs2e if even else rs2o
                send(RS2, k, buf.at[k // 2, 0, q], dst.at[k // 2, peers - 1 - i], (target, f))

        by_parity(k, go)

    def stage2(k):
        def go(even):
            wait_bytes(recv_sem, RS2, k, amount(RS2, k, even))
            one, two = (rs1e, rs2e) if even else (rs1o, rs2o)
            ones, twos = (B - 1, A - 1) if even else (A - 1, B - 1)
            q = a if even else b

            def add(j, carry):
                total = f32(delta[k, r, rows(j), :])
                for s in range(ones):
                    total = total + f32(one[k // 2, s, q, rows(j), :])
                for s in range(twos):
                    total = total + f32(two[k // 2, s, rows(j), :])
                part[k, rows(j), :] = total.astype(jnp.bfloat16)
                return carry

            lax.fori_loop(0, F, add, 0, unroll=4)

        by_parity(k, go)

        def out(i, carry):
            j = f_peer(i)
            send(X1, k, part.at[k, rows(j)], got.at[k, rows(f)], (r, j))
            return carry

        lax.fori_loop(0, F - 1, out, 0)
        got[k, rows(f), :] = part[k, rows(f), :]

    def results(k):
        span = pl.ds(pl.multiple_of(k * sub, sub), sub)
        return (
            pltpu.make_async_copy(mast.at[span], new_master.at[span], out_sem.at[0, k]),
            pltpu.make_async_copy(mom.at[span], new_momentum.at[span], out_sem.at[1, k]),
        )

    def own(k):
        return pltpu.make_async_copy(wsend.at[k, rows(f)], weights.at[r * F + f, k], own_sem.at[k])

    def stage3(k):
        @pl.when(k == 0)
        def _():
            for copy in state_in:
                copy.wait()

        wait_bytes(recv_sem, X1, k, amount(X1, k, True))
        span = pl.ds(pl.multiple_of(k * sub, sub), sub)

        def update(j, carry):
            cols = pl.ds(pl.multiple_of(j * width, width), width)
            mean = f32(got[k, rows(j), :]) * (1.0 / R)
            m = momentum_factor * mom[span, cols] + mean
            p = mast[span, cols] - outer_rate * (mean + momentum_factor * m)
            mom[span, cols] = m
            mast[span, cols] = p
            wsend[k, rows(j), :] = p.astype(jnp.bfloat16)
            return carry

        lax.fori_loop(0, F, update, 0, unroll=4)

        def out(i, carry):
            j = f_peer(i)
            send(X2, k, wsend.at[k, rows(j)], weights.at[r * F + f, k], (r, j))
            return carry

        lax.fori_loop(0, F - 1, out, 0)
        own(k).start()
        for copy in results(k):
            copy.start()

    def stage4(k):
        wait_bytes(recv_sem, X2, k, amount(X2, k, True))
        own(k).wait()

        def go(even):
            here = weights.at[pl.ds(r * F, F), k]
            for i in range(B - 1 if even else A - 1):
                target = a * B + b_peer(i) if even else a_peer(i) * B + b
                send(AG1, k, here, here, (target, f))

        by_parity(k, go)

    def stage5(k):
        def go(even):
            wait_bytes(recv_sem, AG1, k, amount(AG1, k, even))
            if even:
                here = weights.at[pl.ds(a * B * F, B * F), k]
                for i in range(A - 1):
                    send(AG2, k, here, here, (a_peer(i) * B + b, f))
            else:
                for i in range(B - 1):
                    for aa in range(A):
                        here = weights.at[pl.ds((aa * B + b) * F, F), k]
                        send(AG2, k, here, here, (a * B + b_peer(i), f))

        by_parity(k, go)

    def stage6(k):
        by_parity(k, lambda even: wait_bytes(recv_sem, AG2, k, amount(AG2, k, even)))

    stages = (stage0, stage1, stage2, stage3, stage4, stage5, stage6)

    def step(t, carry):
        for lag, stage in zip(LAGS, stages):
            k = t - lag

            @pl.when((k >= 0) & (k < K))
            def _():
                stage(k)

        return carry

    lax.fori_loop(0, K + LAGS[-1], step, 0)

    def finish(k, carry):
        for copy in results(k):
            copy.wait()

        def go(even):
            for stage in range(6):
                wait_bytes(send_sem, stage, k, amount(stage, k, even))

        by_parity(k, go)
        return carry

    lax.fori_loop(0, K, finish, 0)


def solution(mesh):
    R, F = mesh.shape["replica"], mesh.shape["fsdp"]
    B = 2
    A = R // B

    def local(codes, scales, master, momentum):
        total_rows, width = codes.shape[1:]
        blocks = scales.shape[1]
        own = total_rows // (R * F)
        sub = 16 if own % 16 == 0 else own
        K = own // sub
        FS = F * sub
        even, odd = (K + 1) // 2, max(1, K // 2)
        codes = codes.reshape(R * F, K, sub, width)
        lines = max(8, blocks)
        any_spec = pl.BlockSpec(memory_space=pl.ANY)
        bf16 = jnp.bfloat16
        new_master, new_momentum, weights = pl.pallas_call(
            functools.partial(kernel, (A, B, F, K, sub, width, blocks)),
            out_shape=(
                pltpu.VMEM(master.shape, jnp.float32),
                pltpu.VMEM(momentum.shape, jnp.float32),
                pltpu.VMEM((R * F, K, sub, width), bf16),
            ),
            in_specs=[any_spec] * 4,
            out_specs=(any_spec,) * 3,
            scratch_shapes=[
                pltpu.VMEM((K, R, FS, width), bf16),
                pltpu.VMEM((even, B - 1, A, FS, width), bf16),
                pltpu.VMEM((odd, A - 1, B, FS, width), bf16),
                pltpu.VMEM((even, A - 1, FS, width), bf16),
                pltpu.VMEM((odd, B - 1, FS, width), bf16),
                pltpu.VMEM((K, FS, width), bf16),
                pltpu.VMEM((K, FS, width), bf16),
                pltpu.VMEM((K, FS, width), bf16),
                pltpu.VMEM(master.shape, jnp.float32),
                pltpu.VMEM(momentum.shape, jnp.float32),
                pltpu.VMEM((2, R * F, sub, width), jnp.int32),
                pltpu.VMEM((lines, total_rows), jnp.float32),
                pltpu.VMEM((total_rows, lines), jnp.float32),
                pltpu.SemaphoreType.DMA((6, K)),
                pltpu.SemaphoreType.DMA((6, K)),
                pltpu.SemaphoreType.DMA((2,)),
                pltpu.SemaphoreType.DMA((3,)),
                pltpu.SemaphoreType.DMA((2, K)),
                pltpu.SemaphoreType.DMA((K,)),
            ],
            compiler_params=pltpu.CompilerParams(
                collective_id=0, has_side_effects=True, vmem_limit_bytes=40 * 1024 * 1024
            ),
        )(codes, scales, master, momentum)
        return (new_master, new_momentum, weights.reshape(total_rows, width))

    return jax.shard_map(
        local,
        mesh=mesh,
        in_specs=(
            P("replica", None, "fsdp"),
            P("replica", "fsdp", None),
            P(("replica", "fsdp"), None),
            P(("replica", "fsdp"), None),
        ),
        out_specs=(P(("replica", "fsdp"), None), P(("replica", "fsdp"), None), P(None, "fsdp")),
        check_vma=False,
    )
```

profile of v0, /device:TPU:27, one launch (start us, length us, event | category | flops | bytes accessed | tf_op | source)
XLA Modules:
  0.0 154.0 jit_solution(5425350073245399194)
XLA Ops:
  0.6 145.9 %shard_map.67 = (f32[256,4096]{1,0:T(8,128)S(1)}, f32[256,4096]{1,0:T(8,128)S(1)}, bf16[32,16,16,512]{3,2,1,0:T(8,128)(2,1)S(1)}) custom-call(s32[32,16,16,512]{3,2,1,0:T(8,128)} %bitcast.3, f32[1,4,8192]{2,1,0:T(4,128)} %scales.1, f32[256,4096]{1,0:T(8,128)} %master.1, f32[256,4096]{1,0:T(8,128)} %momentum.1), custom_call_target="tpu_custom_call" | custom-call | tf_op jit(solution)/shard_map/pallas_call | solution.py:303
  146.5 2.0 %copy.10 = f32[256,4096]{1,0:T(8,128)} copy(f32[256,4096]{1,0:T(8,128)S(1)} %get-tuple-element.9) | data formatting | bytes 8388608
  148.5 2.0 %copy.11 = f32[256,4096]{1,0:T(8,128)} copy(f32[256,4096]{1,0:T(8,128)S(1)} %get-tuple-element.10) | data formatting | bytes 8388608
  150.6 3.4 %copy.12 = bf16[8192,512]{1,0:T(8,128)(2,1)} copy(bf16[8192,512]{1,0:T(8,128)(2,1)S(1)} %bitcast.2) | data formatting | bytes 16777216
where the time goes:
time: 157 us; the launch traced here: 154 us
  Pallas kernels  146 us (93%)
  local copies, waits for them, and re-layouts  7.42 us (5%)
    pallas_call x1, Pallas kernels, local(): pl.pallas_call(functools.partial(kernel, (A, B, F, K, sub, width, blocks)...  146 us
    unnamed x3, local copies, waits for them, and re-layouts  7.42 us

commit v1 on v0

--- a/solution.py
+++ b/solution.py
@@ -12,17 +12,19 @@
 outer_rate = 0.7
 momentum_factor = 0.9
 
-LAGS = (0, 2, 4, 6, 8, 10, 12)
+LAGS = (0, 3, 6, 8, 10, 13, 16)
 RS1, RS2, X1, X2, AG1, AG2 = range(6)
 
 
 def kernel(cfg, codes, scales, master, momentum, new_master, new_momentum, weights,
-           delta, rs1e, rs1o, rs2e, rs2o, part, got, wsend, mast, mom, cbuf, flat, sbuf,
-           send_sem, recv_sem, in_sem, state_sem, out_sem, own_sem):
+           delta, rs1e, rs1o, rs2e, rs2o, part, got, wsend, cbuf, flat, sbuf,
+           send_sem, recv_sem, in_sem, state_sem, near_sem, far_sem):
     A, B, F, K, sub, width, blocks = cfg
-    R, FS, block = A * B, F * sub, width // blocks
+    R, block = A * B, width // blocks
     r, f = lax.axis_index("replica"), lax.axis_index("fsdp")
     a, b = r // B, lax.rem(r, B)
+    odd_core = lax.rem(f, 2)
+    partner = (r, f + 1 - 2 * odd_core)
 
     def a_peer(i):
         return lax.rem(a + 1 + i, A)
@@ -33,38 +35,46 @@
     def f_peer(i):
         return lax.rem(f + 1 + i, F)
 
+    barrier = pltpu.get_barrier_semaphore()
+    near = f - odd_core + 1
+    for i in range(A - 1):
+        pl.semaphore_signal(barrier, inc=1, device_id=(a_peer(i) * B + b, near), device_id_type=MESH)
+    for i in range(B - 1):
+        pl.semaphore_signal(barrier, inc=1, device_id=(a * B + b_peer(i), near), device_id_type=MESH)
+
+    @pl.when(odd_core == 0)
+    def _():
+        pl.semaphore_signal(barrier, inc=1, device_id=partner, device_id_type=MESH)
+
     def load(k):
         slot = lax.rem(k, 2)
-        return (pltpu.make_async_copy(codes.at[:, k], cbuf.at[slot], in_sem.at[slot]),)
+        return tuple(
+            pltpu.make_async_copy(codes.at[pl.ds(q * F, F), k], cbuf.at[slot, pl.ds(q * F, F)], in_sem.at[slot, q])
+            for q in range(R)
+        )
 
     scales_in = pltpu.make_async_copy(scales.at[0], flat.at[pl.ds(0, blocks)], state_sem.at[2])
     scales_in.start()
     for k in range(min(2, K)):
         for copy in load(k):
             copy.start()
+
+    for i in range(F // 2 - 1):
+        pair = lax.rem(f // 2 + 1 + i, F // 2)
+        pl.semaphore_signal(barrier, inc=1, device_id=(r, 2 * pair), device_id_type=MESH)
+
     state_in = (
-        pltpu.make_async_copy(master, mast, state_sem.at[0]),
-        pltpu.make_async_copy(momentum, mom, state_sem.at[1]),
+        pltpu.make_async_copy(master, new_master, state_sem.at[0]),
+        pltpu.make_async_copy(momentum, new_momentum, state_sem.at[1]),
     )
-    for copy in state_in:
-        copy.start()
-
-    barrier = pltpu.get_barrier_semaphore()
-    for i in range(A - 1):
-        pl.semaphore_signal(barrier, inc=1, device_id=(a_peer(i) * B + b, f), device_id_type=MESH)
-    for i in range(B - 1):
-        pl.semaphore_signal(barrier, inc=1, device_id=(a * B + b_peer(i), f), device_id_type=MESH)
-    for i in range(F - 1):
-        pl.semaphore_signal(barrier, inc=1, device_id=(r, f_peer(i)), device_id_type=MESH)
-    scales_in.wait()
 
     def turn(i, carry):
         tile = flat[:, pl.ds(pl.multiple_of(i * 128, 128), 128)]
         sbuf[pl.ds(pl.multiple_of(i * 128, 128), 128), :] = jnp.transpose(tile)
         return carry
 
+    scales_in.wait()
     lax.fori_loop(0, flat.shape[1] // 128, turn, 0, unroll=8)
-    pl.semaphore_wait(barrier, A + B + F - 3)
 
     def send(stage, k, src, dst, device):
         pltpu.make_async_remote_copy(
@@ -102,7 +112,7 @@
             def _():
                 fn(False)
 
-    def stage0(k):
+    def scale_codes(k):
         slot = lax.rem(k, 2)
         for copy in load(k):
             copy.wait()
@@ -117,11 +127,7 @@
 
         lax.fori_loop(0, R * F, one, 0, unroll=4)
 
-        @pl.when(k + 2 < K)
-        def _():
-            for copy in load(k + 2):
-                copy.start()
-
+    def send_first(k):
         def go(even):
             if even:
                 for i in range(B - 1):
@@ -135,6 +141,23 @@
 
         by_parity(k, go)
 
+    def stage0(k):
+        @pl.when(k > 0)
+        def _():
+            scale_codes(k)
+
+        send_first(k)
+
+        @pl.when(k == 0)
+        def _():
+            for copy in state_in:
+                copy.start()
+
+        @pl.when(k + 2 < K)
+        def _():
+            for copy in load(k + 2):
+                copy.start()
+
     def stage1(k):
         def go(even):
             wait_bytes(recv_sem, RS1, k, amount(RS1, k, even))
@@ -176,6 +199,15 @@
 
         by_parity(k, go)
 
+        @pl.when((k == 0) & (odd_core == 0))
+        def _():
+            pl.semaphore_wait(barrier, F - 2)
+            pl.semaphore_signal(far_sem, inc=1, device_id=partner, device_id_type=MESH)
+
+        @pl.when((k == 0) & (odd_core == 1))
+        def _():
+            pl.semaphore_wait(far_sem, 1)
+
         def out(i, carry):
             j = f_peer(i)
             send(X1, k, part.at[k, rows(j)], got.at[k, rows(f)], (r, j))
@@ -184,16 +216,6 @@
         lax.fori_loop(0, F - 1, out, 0)
         got[k, rows(f), :] = part[k, rows(f), :]
 
-    def results(k):
-        span = pl.ds(pl.multiple_of(k * sub, sub), sub)
-        return (
-            pltpu.make_async_copy(mast.at[span], new_master.at[span], out_sem.at[0, k]),
-            pltpu.make_async_copy(mom.at[span], new_momentum.at[span], out_sem.at[1, k]),
-        )
-
-    def own(k):
-        return pltpu.make_async_copy(wsend.at[k, rows(f)], weights.at[r * F + f, k], own_sem.at[k])
-
     def stage3(k):
         @pl.when(k == 0)
         def _():
@@ -206,10 +228,10 @@
         def update(j, carry):
             cols = pl.ds(pl.multiple_of(j * width, width), width)
             mean = f32(got[k, rows(j), :]) * (1.0 / R)
-            m = momentum_factor * mom[span, cols] + mean
-            p = mast[span, cols] - outer_rate * (mean + momentum_factor * m)
-            mom[span, cols] = m
-            mast[span, cols] = p
+            m = momentum_factor * new_momentum[span, cols] + mean
+            p = new_master[span, cols] - outer_rate * (mean + momentum_factor * m)
+            new_momentum[span, cols] = m
+            new_master[span, cols] = p
             wsend[k, rows(j), :] = p.astype(jnp.bfloat16)
             return carry
 
@@ -221,13 +243,10 @@
             return carry
 
         lax.fori_loop(0, F - 1, out, 0)
-        own(k).start()
-        for copy in results(k):
-            copy.start()
+        weights[r * F + f, k, :, :] = wsend[k, rows(f), :]
 
     def stage4(k):
         wait_bytes(recv_sem, X2, k, amount(X2, k, True))
-        own(k).wait()
 
         def go(even):
             here = weights.at[pl.ds(r * F, F), k]
@@ -253,7 +272,13 @@
         by_parity(k, go)
 
     def stage6(k):
-        by_parity(k, lambda even: wait_bytes(recv_sem, AG2, k, amount(AG2, k, even)))
+        def go(even):
+            for stage in range(5):
+                wait_bytes(send_sem, stage, k, amount(stage, k, even))
+            wait_bytes(recv_sem, AG2, k, amount(AG2, k, even))
+            wait_bytes(send_sem, AG2, k, amount(AG2, k, even))
+
+        by_parity(k, go)
 
     stages = (stage0, stage1, stage2, stage3, stage4, stage5, stage6)
 
@@ -267,20 +292,28 @@
 
         return carry
 
+    scale_codes(0)
+
+    @pl.when(odd_core == 1)
+    def _():
+        pl.semaphore_wait(barrier, 2 * (A + B - 2) + 1)
+        pl.semaphore_signal(near_sem, inc=1, device_id=partner, device_id_type=MESH)
+
+    @pl.when(odd_core == 0)
+    def _():
+        pl.semaphore_wait(near_sem, 1)
+
     lax.fori_loop(0, K + LAGS[-1], step, 0)
 
-    def finish(k, carry):
-        for copy in results(k):
-            copy.wait()
-
-        def go(even):
-            for stage in range(6):
-                wait_bytes(send_sem, stage, k, amount(stage, k, even))
-
-        by_parity(k, go)
-        return carry
-
-    lax.fori_loop(0, K, finish, 0)
+
+def put(sources, targets, sem):
+    copies = [
+        pltpu.make_async_copy(source, target, sem.at[n]) for n, (source, target) in enumerate(zip(sources, targets))
+    ]
+    for copy in copies:
+        copy.start()
+    for copy in copies:
+        copy.wait()
 
 
 def solution(mesh):
@@ -299,16 +332,18 @@
         codes = codes.reshape(R * F, K, sub, width)
         lines = max(8, blocks)
         any_spec = pl.BlockSpec(memory_space=pl.ANY)
+        hbm_spec = pl.BlockSpec(memory_space=pltpu.HBM)
         bf16 = jnp.bfloat16
-        new_master, new_momentum, weights = pl.pallas_call(
+        state, layout = master.shape, (R * F, K, sub, width)
+        results = pl.pallas_call(
             functools.partial(kernel, (A, B, F, K, sub, width, blocks)),
             out_shape=(
-                pltpu.VMEM(master.shape, jnp.float32),
-                pltpu.VMEM(momentum.shape, jnp.float32),
-                pltpu.VMEM((R * F, K, sub, width), bf16),
+                pltpu.VMEM(state, jnp.float32),
+                pltpu.VMEM(state, jnp.float32),
+                pltpu.VMEM(layout, bf16),
             ),
-            in_specs=[any_spec] * 4,
-            out_specs=(any_spec,) * 3,
+            in_specs=[hbm_spec] * 4,
+            out_specs=(pl.BlockSpec(memory_space=pltpu.VMEM),) * 3,
             scratch_shapes=[
                 pltpu.VMEM((K, R, FS, width), bf16),
                 pltpu.VMEM((even, B - 1, A, FS, width), bf16),
@@ -318,22 +353,32 @@
                 pltpu.VMEM((K, FS, width), bf16),
                 pltpu.VMEM((K, FS, width), bf16),
                 pltpu.VMEM((K, FS, width), bf16),
-                pltpu.VMEM(master.shape, jnp.float32),
-                pltpu.VMEM(momentum.shape, jnp.float32),
                 pltpu.VMEM((2, R * F, sub, width), jnp.int32),
                 pltpu.VMEM((lines, total_rows), jnp.float32),
                 pltpu.VMEM((total_rows, lines), jnp.float32),
                 pltpu.SemaphoreType.DMA((6, K)),
                 pltpu.SemaphoreType.DMA((6, K)),
-                pltpu.SemaphoreType.DMA((2,)),
+                pltpu.SemaphoreType.DMA((2, R)),
                 pltpu.SemaphoreType.DMA((3,)),
-                pltpu.SemaphoreType.DMA((2, K)),
-                pltpu.SemaphoreType.DMA((K,)),
+                pltpu.SemaphoreType.REGULAR,
+                pltpu.SemaphoreType.REGULAR,
             ],
             compiler_params=pltpu.CompilerParams(
-                collective_id=0, has_side_effects=True, vmem_limit_bytes=40 * 1024 * 1024
+                collective_id=0, has_side_effects=True, vmem_limit_bytes=36 * 1024 * 1024
             ),
         )(codes, scales, master, momentum)
+        new_master, new_momentum, weights = pl.pallas_call(
+            lambda *refs: put(refs[:3], refs[3:6], refs[6]),
+            out_shape=(
+                jax.ShapeDtypeStruct(state, jnp.float32),
+                jax.ShapeDtypeStruct(state, jnp.float32),
+                jax.ShapeDtypeStruct(layout, bf16),
+            ),
+            in_specs=[any_spec] * 3,
+            out_specs=(hbm_spec,) * 3,
+            scratch_shapes=[pltpu.SemaphoreType.DMA((3,))],
+            compiler_params=pltpu.CompilerParams(vmem_limit_bytes=1024 * 1024),
+        )(*results)
         return (new_master, new_momentum, weights.reshape(total_rows, width))
 
     return jax.shard_map(

time: 157 us -> 152 us (0.968)
  local copies, waits for them, and re-layouts: 7.42 us -> 0.9 us
  Pallas kernels: 146 us -> 148 us
    unnamed x3 -> x2, local copies, waits for them, and re-layouts: 7.42 us -> 0.9 us
    pallas_call x0 -> x1, Pallas kernels: none -> 6.07 us  [local(): pl.pallas_call(lambda *refs: put(refs[:3], refs[3:6], refs[6]), out_shape...]
    pallas_call x1, Pallas kernels: 146 us -> 142 us  [local(): pl.pallas_call(functools.partial(kernel, (A, B, F, K, sub, width, blocks)...]
where the time goes in v1:
time: 152 us; the launch traced here: 150 us
  Pallas kernels  148 us (97%)
    pallas_call x1, Pallas kernels, local(): pl.pallas_call(functools.partial(kernel, (A, B, F, K, sub, width, blocks)...  142 us
    pallas_call x1, Pallas kernels, local(): pl.pallas_call(lambda *refs: put(refs[:3], refs[3:6], refs[6]), out_shape...  6.07 us

profile of v1, /device:TPU:27, one launch (start us, length us, event | category | flops | bytes accessed | tf_op | source)
XLA Modules:
  0.0 149.7 jit_solution(10447563444328170021)
XLA Ops:
  0.6 0.0 copy-start
  0.6 0.9 copy-done
  1.5 142.1 %shard_map.67 = (f32[256,4096]{1,0:T(8,128)S(1)}, f32[256,4096]{1,0:T(8,128)S(1)}, bf16[32,16,16,512]{3,2,1,0:T(8,128)(2,1)S(1)}) custom-call(s32[32,16,16,512]{3,2,1,0:T(8,128)} %bitcast.2, f32[1,4,8192]{2,1,0:T(4,128)S(1)} %copy-done, f32[256,4096]{1,0:T(8,128)} %master.1, f32[256,4096]{1,0:T(8,128)} %momentum.1), custom_call_target="tpu_custom_call" | custom-call | tf_op jit(solution)/shard_map/pallas_call | solution.py:338
  143.6 6.1 %shard_map.68 = (f32[256,4096]{1,0:T(8,128)}, f32[256,4096]{1,0:T(8,128)}, bf16[32,16,16,512]{3,2,1,0:T(8,128)(2,1)}) custom-call(f32[256,4096]{1,0:T(8,128)S(1)} %get-tuple-element.9.refs_0_, f32[256,4096]{1,0:T(8,128)S(1)} %get-tuple-element.10.refs_1_, bf16[32,16,16,512]{3,2,1,0:T(8,128)(2,1)S(1)} %get-tuple-element.11.refs_2_), custom_call_target="tpu_custom_call" | custom-call | tf_op jit(solution)/shard_map/pallas_call | solution.py:370
Async XLA Ops:
  0.6 0.9 copy-start

commit v2 on v1

--- a/solution.py
+++ b/solution.py
@@ -18,9 +18,9 @@
 
 def kernel(cfg, codes, scales, master, momentum, new_master, new_momentum, weights,
            delta, rs1e, rs1o, rs2e, rs2o, part, got, wsend, cbuf, flat, sbuf,
-           send_sem, recv_sem, in_sem, state_sem, near_sem, far_sem):
+           send_sem, recv_sem, in_sem, scale_sem, state_sem, near_sem, far_sem):
     A, B, F, K, sub, width, blocks = cfg
-    R, block = A * B, width // blocks
+    R, block, own = A * B, width // blocks, K * sub
     r, f = lax.axis_index("replica"), lax.axis_index("fsdp")
     a, b = r // B, lax.rem(r, B)
     odd_core = lax.rem(f, 2)
@@ -46,18 +46,32 @@
     def _():
         pl.semaphore_signal(barrier, inc=1, device_id=partner, device_id_type=MESH)
 
-    def load(k):
-        slot = lax.rem(k, 2)
-        return tuple(
-            pltpu.make_async_copy(codes.at[pl.ds(q * F, F), k], cbuf.at[slot, pl.ds(q * F, F)], in_sem.at[slot, q])
-            for q in range(R)
-        )
-
-    scales_in = pltpu.make_async_copy(scales.at[0], flat.at[pl.ds(0, blocks)], state_sem.at[2])
-    scales_in.start()
-    for k in range(min(2, K)):
-        for copy in load(k):
-            copy.start()
+    def offsets(even, p):
+        if even:
+            return lax.rem(1 + lax.rem(p, A), A), lax.rem(1 + p // A, B)
+        return lax.rem(1 + p // B, A), lax.rem(1 + lax.rem(p, B), B)
+
+    def at(da, db):
+        return lax.rem(a + da, A) * B + lax.rem(b + db, B)
+
+    def load(k, q):
+        slot, group = lax.rem(k, 2), pl.ds(q * F, F)
+        return pltpu.make_async_copy(codes.at[group, k], cbuf.at[slot, group], in_sem.at[slot, q])
+
+    def scales_in(q):
+        group = pl.ds(q * F * own, F * own)
+        return pltpu.make_async_copy(scales.at[0, :, group], flat.at[pl.ds(0, blocks), group], scale_sem.at[q])
+
+    first = tuple(
+        (k, p, ((1 + p % A) % A, (1 + p // A) % B) if k == 0 else ((1 + p // B) % A, (1 + p % B) % B))
+        for p in range(R) for k in range(min(2, K))
+    )
+    seen = set()
+    for k, p, spot in first:
+        if spot not in seen:
+            seen.add(spot)
+            scales_in(at(*spot)).start()
+        load(k, at(*spot)).start()
 
     for i in range(F // 2 - 1):
         pair = lax.rem(f // 2 + 1 + i, F // 2)
@@ -68,13 +82,9 @@
         pltpu.make_async_copy(momentum, new_momentum, state_sem.at[1]),
     )
 
-    def turn(i, carry):
-        tile = flat[:, pl.ds(pl.multiple_of(i * 128, 128), 128)]
-        sbuf[pl.ds(pl.multiple_of(i * 128, 128), 128), :] = jnp.transpose(tile)
-        return carry
-
-    scales_in.wait()
-    lax.fori_loop(0, flat.shape[1] // 128, turn, 0, unroll=8)
+    def turn(i):
+        span = pl.ds(pl.multiple_of(i * 128, 128), 128)
+        sbuf[span, :] = jnp.transpose(flat[:, span])
 
     def send(stage, k, src, dst, device):
         pltpu.make_async_remote_copy(
@@ -112,51 +122,90 @@
             def _():
                 fn(False)
 
-    def scale_codes(k):
+    def turn_scales(k, q):
+        each, tiles = (F, own // 128) if own % 128 == 0 else (F * own // 128, 1)
+        part = k * sub // 128 if own % 128 == 0 else 0
+
+        def some(j, carry):
+            turn((q * each + j) * tiles + part)
+            return carry
+
+        lax.fori_loop(0, each, some, 0, unroll=8)
+
+    def scale_piece(k, q):
         slot = lax.rem(k, 2)
-        for copy in load(k):
-            copy.wait()
-
-        def one(g, carry):
-            q, j = g // F, lax.rem(g, F)
+        load(k, q).wait()
+
+        def one(j, carry):
+            g = q * F + j
             for n in range(blocks):
                 cols = pl.ds(n * block, block)
-                value = f32(cbuf[slot, g, :, cols]) * sbuf[pl.ds(pl.multiple_of((g * K + k) * sub, sub), sub), pl.ds(n, 1)]
+                value = f32(cbuf[slot, g, :, cols]) * sbuf[rows(g * K + k), pl.ds(n, 1)]
                 delta[k, q, rows(j), cols] = value.astype(jnp.bfloat16)
             return carry
 
-        lax.fori_loop(0, R * F, one, 0, unroll=4)
-
-    def send_first(k):
-        def go(even):
-            if even:
-                for i in range(B - 1):
-                    bb = b_peer(i)
-                    for aa in range(A):
-                        send(RS1, k, delta.at[k, aa * B + bb], rs1e.at[k // 2, B - 2 - i, aa], (a * B + bb, f))
-            else:
-                for i in range(A - 1):
-                    aa = a_peer(i)
-                    send(RS1, k, delta.at[k, pl.ds(aa * B, B)], rs1o.at[k // 2, A - 2 - i], (aa * B + b, f))
-
-        by_parity(k, go)
-
-    def stage0(k):
-        @pl.when(k > 0)
-        def _():
-            scale_codes(k)
-
-        send_first(k)
-
-        @pl.when(k == 0)
-        def _():
-            for copy in state_in:
-                copy.start()
-
+        lax.fori_loop(0, F, one, 0, unroll=4)
+
+    def send_even(k, p, q):
+        i, aa = p // A, q // B
+        send(RS1, k, delta.at[k, q], rs1e.at[k // 2, B - 2 - i, aa], (a * B + lax.rem(q, B), f))
+
+    def send_odd(k, p, q):
+        i, bb = p // B, lax.rem(q, B)
+        send(RS1, k, delta.at[k, q], rs1o.at[k // 2, A - 2 - i, bb], ((q // B) * B + b, f))
+
+    def refill(k):
         @pl.when(k + 2 < K)
         def _():
-            for copy in load(k + 2):
-                copy.start()
+            for q in range(R):
+                load(k + 2, q).start()
+
+    def begin():
+        seen = set()
+        for n, (k, p, spot) in enumerate(first):
+            q = at(*spot)
+            if spot not in seen:
+                seen.add(spot)
+                scales_in(q).wait()
+                turn_scales(0, q)
+            scale_piece(k, q)
+            if n == 0:
+                @pl.when(odd_core == 1)
+                def _():
+                    pl.semaphore_wait(barrier, 2 * (A + B - 2) + 1)
+                    pl.semaphore_signal(near_sem, inc=1, device_id=partner, device_id_type=MESH)
+
+                @pl.when(odd_core == 0)
+                def _():
+                    pl.semaphore_wait(near_sem, 1)
+
+            if k == 0 and p < A * (B - 1):
+                send_even(k, p, q)
+            if k == 1 and p < B * (A - 1):
+                send_odd(k, p, q)
+        for k in range(min(2, K)):
+            refill(k)
+        for copy in state_in:
+            copy.start()
+
+    def stage0(k):
+        def piece(even, p, carry):
+            q = at(*offsets(even, p))
+            if own % 128 == 0:
+                @pl.when(lax.rem(k, 128 // sub) == 0)
+                def _():
+                    turn_scales(k, q)
+
+            scale_piece(k, q)
+
+            @pl.when(p < (A * (B - 1) if even else B * (A - 1)))
+            def _():
+                (send_even if even else send_odd)(k, p, q)
+
+            return carry
+
+        by_parity(k, lambda even: lax.fori_loop(0, R, functools.partial(piece, even), 0))
+        refill(k)
 
     def stage1(k):
         def go(even):
@@ -286,23 +335,13 @@
         for lag, stage in zip(LAGS, stages):
             k = t - lag
 
-            @pl.when((k >= 0) & (k < K))
+            @pl.when((k >= (min(2, K) if stage is stage0 else 0)) & (k < K))
             def _():
                 stage(k)
 
         return carry
 
-    scale_codes(0)
-
-    @pl.when(odd_core == 1)
-    def _():
-        pl.semaphore_wait(barrier, 2 * (A + B - 2) + 1)
-        pl.semaphore_signal(near_sem, inc=1, device_id=partner, device_id_type=MESH)
-
-    @pl.when(odd_core == 0)
-    def _():
-        pl.semaphore_wait(near_sem, 1)
-
+    begin()
     lax.fori_loop(0, K + LAGS[-1], step, 0)
 
 
@@ -359,12 +398,13 @@
                 pltpu.SemaphoreType.DMA((6, K)),
                 pltpu.SemaphoreType.DMA((6, K)),
                 pltpu.SemaphoreType.DMA((2, R)),
-                pltpu.SemaphoreType.DMA((3,)),
+                pltpu.SemaphoreType.DMA((R,)),
+                pltpu.SemaphoreType.DMA((2,)),
                 pltpu.SemaphoreType.REGULAR,
                 pltpu.SemaphoreType.REGULAR,
             ],
             compiler_params=pltpu.CompilerParams(
-                collective_id=0, has_side_effects=True, vmem_limit_bytes=36 * 1024 * 1024
+                collective_id=0, has_side_effects=True, vmem_limit_bytes=46 * 1024 * 1024
             ),
         )(codes, scales, master, momentum)
         new_master, new_momentum, weights = pl.pallas_call(

time: 152 us -> 149 us (0.980)
    pallas_call x1, Pallas kernels: 142 us -> 141 us  [local(): pl.pallas_call(functools.partial(kernel, (A, B, F, K, sub, width, blocks)...]
where the time goes in v2:
time: 149 us; the launch traced here: 147 us
  Pallas kernels  147 us (99%)
    pallas_call x1, Pallas kernels, local(): pl.pallas_call(functools.partial(kernel, (A, B, F, K, sub, width, blocks)...  141 us
    pallas_call x1, Pallas kernels, local(): pl.pallas_call(lambda *refs: put(refs[:3], refs[3:6], refs[6]), out_shape...  6.07 us

profile of v2, /device:TPU:27, one launch (start us, length us, event | category | flops | bytes accessed | tf_op | source)
XLA Modules:
  0.0 147.2 jit_solution(14264744850335612220)
XLA Ops:
  0.6 140.5 %shard_map.67 = (f32[256,4096]{1,0:T(8,128)S(1)}, f32[256,4096]{1,0:T(8,128)S(1)}, bf16[32,16,16,512]{3,2,1,0:T(8,128)(2,1)S(1)}) custom-call(s32[32,16,16,512]{3,2,1,0:T(8,128)} %bitcast.2, f32[1,4,8192]{2,1,0:T(4,128)} %scales.1, f32[256,4096]{1,0:T(8,128)} %master.1, f32[256,4096]{1,0:T(8,128)} %momentum.1), custom_call_target="tpu_custom_call" | custom-call | tf_op jit(solution)/shard_map/pallas_call | solution.py:377
  141.1 6.1 %shard_map.68 = (f32[256,4096]{1,0:T(8,128)}, f32[256,4096]{1,0:T(8,128)}, bf16[32,16,16,512]{3,2,1,0:T(8,128)(2,1)}) custom-call(f32[256,4096]{1,0:T(8,128)S(1)} %get-tuple-element.9.refs_0_, f32[256,4096]{1,0:T(8,128)S(1)} %get-tuple-element.10.refs_1_, bf16[32,16,16,512]{3,2,1,0:T(8,128)(2,1)S(1)} %get-tuple-element.11.refs_2_), custom_call_target="tpu_custom_call" | custom-call | tf_op jit(solution)/shard_map/pallas_call | solution.py:410

commit v3 on v2

--- a/solution.py
+++ b/solution.py
@@ -12,18 +12,39 @@
 outer_rate = 0.7
 momentum_factor = 0.9
 
-LAGS = (0, 3, 6, 8, 10, 13, 16)
+LAGS = (0, 3, 6, 8, 10, 13, 13, 16)
+EARLY = (8, 10, 16)
+LONG = 0
+TAIL = 10
 RS1, RS2, X1, X2, AG1, AG2 = range(6)
+
+
+def spread(even, A, B, F, a, b):
+    if even:
+        return [(pl.ds(a * B * F, B * F), i, pl.ds((A - 2 - i) * B * F, B * F)) for i in range(A - 1)]
+    return [
+        (pl.ds((aa * B + b) * F, F), i, pl.ds(((B - 2 - i) * A + aa) * F, F)) for i in range(B - 1) for aa in range(A)
+    ]
+
+
+def gathered(even, A, B, F, a, b):
+    if even:
+        return [(pl.ds(i * B * F, B * F), pl.ds(lax.rem(a + 1 + i, A) * B * F, B * F)) for i in range(A - 1)]
+    return [
+        (pl.ds((i * A + aa) * F, F), pl.ds((aa * B + lax.rem(b + 1 + i, B)) * F, F)) for i in range(B - 1) for aa in range(A)
+    ]
 
 
 def kernel(cfg, codes, scales, master, momentum, new_master, new_momentum, weights,
            delta, rs1e, rs1o, rs2e, rs2o, part, got, wsend, cbuf, flat, sbuf,
            send_sem, recv_sem, in_sem, scale_sem, state_sem, near_sem, far_sem):
-    A, B, F, K, sub, width, blocks = cfg
+    A, B, F, K, sub, width, blocks, late = cfg
     R, block, own = A * B, width // blocks, K * sub
     r, f = lax.axis_index("replica"), lax.axis_index("fsdp")
     a, b = r // B, lax.rem(r, B)
     odd_core = lax.rem(f, 2)
+    held = jnp.where(odd_core == LONG, late[1], late[0])
+    spread_out = jnp.where(odd_core == LONG, late[2], late[0])
     partner = (r, f + 1 - 2 * odd_core)
 
     def a_peer(i):
@@ -306,30 +327,42 @@
         by_parity(k, go)
 
     def stage5(k):
+        by_parity(k, lambda even: wait_bytes(recv_sem, AG1, k, amount(AG1, k, even)))
+
+    def gather_on(k):
         def go(even):
-            wait_bytes(recv_sem, AG1, k, amount(AG1, k, even))
-            if even:
-                here = weights.at[pl.ds(a * B * F, B * F), k]
-                for i in range(A - 1):
-                    send(AG2, k, here, here, (a_peer(i) * B + b, f))
-            else:
-                for i in range(B - 1):
-                    for aa in range(A):
-                        here = weights.at[pl.ds((aa * B + b) * F, F), k]
-                        send(AG2, k, here, here, (a * B + b_peer(i), f))
+            for source, i, spot in spread(even, A, B, F, a, b):
+                here = weights.at[source, k]
+                send(AG2, k, here, here, ((a_peer(i) * B + b, f) if even else (a * B + b_peer(i), f)))
 
         by_parity(k, go)
 
+    def gather_end(k):
+        def go(even):
+            wait_bytes(recv_sem, AG2, k, amount(AG2, k, even))
+            wait_bytes(send_sem, AG2, k, amount(AG2, k, even))
+
+        by_parity(k, go)
+
     def stage6(k):
+        pl.when((k < spread_out) | ((k > K - 1 + TAIL - LAGS[6]) & (k < held)))(lambda: gather_on(k))
+
+    def stage7(k):
         def go(even):
             for stage in range(5):
                 wait_bytes(send_sem, stage, k, amount(stage, k, even))
-            wait_bytes(recv_sem, AG2, k, amount(AG2, k, even))
-            wait_bytes(send_sem, AG2, k, amount(AG2, k, even))
 
         by_parity(k, go)
-
-    stages = (stage0, stage1, stage2, stage3, stage4, stage5, stage6)
+        pl.when(k < spread_out)(lambda: gather_end(k))
+
+    stages = (stage0, stage1, stage2, stage3, stage4, stage5, stage6, stage7)
+
+    def loop(fn, end):
+        def one(k, carry):
+            fn(k)
+            return carry
+
+        lax.fori_loop(spread_out, end, one, 0)
 
     def step(t, carry):
         for lag, stage in zip(LAGS, stages):
@@ -339,20 +372,107 @@
             def _():
                 stage(k)
 
+        @pl.when(t == K - 1 + TAIL)
+        def _():
+            loop(gather_on, jnp.minimum(held, max(0, K + TAIL - LAGS[6])))
+
         return carry
 
     begin()
     lax.fori_loop(0, K + LAGS[-1], step, 0)
-
-
-def put(sources, targets, sem):
+    loop(gather_end, held)
+
+
+def position(cfg):
+    A, B, F, K, late = cfg
+    r, f = lax.axis_index("replica"), lax.axis_index("fsdp")
+    return r // B, lax.rem(r, B), f, jnp.where(lax.rem(f, 2) == LONG, late[1], late[0])
+
+
+def gather_late(cfg, weights, token, tail, send_sem, recv_sem):
+    A, B, F, K, late = cfg
+    a, b, f, held = position(cfg)
+    barrier = pltpu.get_barrier_semaphore()
+    peers = [(lax.rem(a + 1 + i, A) * B + b, f) for i in range(A - 1)]
+    peers += [(a * B + lax.rem(b + 1 + i, B), f) for i in range(B - 1)]
+    for peer in peers:
+        pl.semaphore_signal(barrier, inc=1, device_id=peer, device_id_type=MESH)
+    pl.semaphore_wait(barrier, A + B - 2)
+
+    def each(fn):
+        def one(k, carry):
+            for even in (True, False):
+                @pl.when(lax.rem(k, 2) == (0 if even else 1))
+                def _():
+                    fn(k, even)
+
+            return carry
+
+        lax.fori_loop(held, K, one, 0)
+
+    def start(k, even):
+        for source, i, slot in spread(even, A, B, F, a, b):
+            pltpu.make_async_remote_copy(
+                src_ref=weights.at[source, k], dst_ref=tail.at[k - min(late[:2]), slot],
+                send_sem=send_sem.at[k], recv_sem=recv_sem.at[k],
+                device_id=peers[i] if even else peers[A - 1 + i], device_id_type=MESH,
+            ).start()
+
+    def finish(k, even):
+        moved = tail.at[k - min(late[:2]), pl.ds(0, ((A - 1) * B if even else A * (B - 1)) * F)]
+        pltpu.make_async_copy(moved, moved, recv_sem.at[k]).wait()
+        pltpu.make_async_copy(moved, moved, send_sem.at[k]).wait()
+
+    each(start)
+    each(finish)
+
+
+def write_early(cfg, master, momentum, weights, new_master, new_momentum, written, token, state_sem, sem, late_sem):
+    A, B, F, K, late = cfg
+    a, b, f, held = position(cfg)
     copies = [
-        pltpu.make_async_copy(source, target, sem.at[n]) for n, (source, target) in enumerate(zip(sources, targets))
+        pltpu.make_async_copy(master, new_master, state_sem.at[0]),
+        pltpu.make_async_copy(momentum, new_momentum, state_sem.at[1]),
     ]
     for copy in copies:
         copy.start()
+
+    def each(act):
+        for k in range(K):
+            if k < max(late[:2]):
+                def whole(k=k):
+                    act(pltpu.make_async_copy(weights.at[:, k], written.at[:, k], sem.at[k]))
+
+                pl.when(k < held)(whole)
+            if k >= min(late[:2]):
+                def mine(k=k):
+                    group = [pl.ds(a * B * F, B * F)] if k % 2 == 0 else [pl.ds((aa * B + b) * F, F) for aa in range(A)]
+                    for n, blocks in enumerate(group):
+                        act(pltpu.make_async_copy(weights.at[blocks, k], written.at[blocks, k], late_sem.at[k, n]))
+
+                pl.when(k >= held)(mine)
+
+    each(lambda copy: copy.start())
+    token[...] = jnp.zeros_like(token)
+    each(lambda copy: copy.wait())
     for copy in copies:
         copy.wait()
+
+
+def write_late(cfg, written, tail, weights, sem):
+    A, B, F, K, late = cfg
+    a, b, f, held = position(cfg)
+
+    def each(act):
+        for k in range(min(late[:2]), K):
+            def piece(k=k):
+                for n, (slot, blocks) in enumerate(gathered(k % 2 == 0, A, B, F, a, b)):
+                    act(pltpu.make_async_copy(tail.at[k - min(late[:2]), slot], weights.at[blocks, k], sem.at[k, n]))
+
+            pl.when(k >= held)(piece)
+
+    each(lambda copy: copy.start())
+    each(lambda copy: copy.wait())
 
 
 def solution(mesh):
@@ -373,9 +493,10 @@
         any_spec = pl.BlockSpec(memory_space=pl.ANY)
         hbm_spec = pl.BlockSpec(memory_space=pltpu.HBM)
         bf16 = jnp.bfloat16
+        late = (K * EARLY[0] // 16, K * EARLY[2] // 16, K * EARLY[1] // 16)
         state, layout = master.shape, (R * F, K, sub, width)
-        results = pl.pallas_call(
-            functools.partial(kernel, (A, B, F, K, sub, width, blocks)),
+        new_master, new_momentum, gathered_early = pl.pallas_call(
+            functools.partial(kernel, (A, B, F, K, sub, width, blocks, late)),
             out_shape=(
                 pltpu.VMEM(state, jnp.float32),
                 pltpu.VMEM(state, jnp.float32),
@@ -407,18 +528,41 @@
                 collective_id=0, has_side_effects=True, vmem_limit_bytes=46 * 1024 * 1024
             ),
         )(codes, scales, master, momentum)
-        new_master, new_momentum, weights = pl.pallas_call(
-            lambda *refs: put(refs[:3], refs[3:6], refs[6]),
+        small = dict(vmem_limit_bytes=1024 * 1024)
+        plan = (A, B, F, K, late)
+        new_master, new_momentum, written, token = pl.pallas_call(
+            functools.partial(write_early, plan),
             out_shape=(
                 jax.ShapeDtypeStruct(state, jnp.float32),
                 jax.ShapeDtypeStruct(state, jnp.float32),
                 jax.ShapeDtypeStruct(layout, bf16),
+                jax.ShapeDtypeStruct((8, 128), jnp.float32),
             ),
             in_specs=[any_spec] * 3,
-            out_specs=(hbm_spec,) * 3,
-            scratch_shapes=[pltpu.SemaphoreType.DMA((3,))],
-            compiler_params=pltpu.CompilerParams(vmem_limit_bytes=1024 * 1024),
-        )(*results)
+            out_specs=(hbm_spec,) * 3 + (pl.BlockSpec(memory_space=pltpu.VMEM),),
+            scratch_shapes=[
+                pltpu.SemaphoreType.DMA((2,)), pltpu.SemaphoreType.DMA((K,)), pltpu.SemaphoreType.DMA((K, A)),
+            ],
+            compiler_params=pltpu.CompilerParams(**small),
+        )(new_master, new_momentum, gathered_early)
+        slots = max((A - 1) * B, A * (B - 1)) * F
+        tail = pl.pallas_call(
+            functools.partial(gather_late, plan),
+            out_shape=pltpu.VMEM((K - min(late[:2]), slots, sub, width), bf16),
+            in_specs=[any_spec] * 2,
+            out_specs=any_spec,
+            scratch_shapes=[pltpu.SemaphoreType.DMA((K,)), pltpu.SemaphoreType.DMA((K,))],
+            compiler_params=pltpu.CompilerParams(collective_id=1, has_side_effects=True, **small),
+        )(gathered_early, token)
+        weights = pl.pallas_call(
+            functools.partial(write_late, plan),
+            out_shape=jax.ShapeDtypeStruct(layout, bf16),
+            in_specs=[hbm_spec, any_spec],
+            out_specs=hbm_spec,
+            input_output_aliases={0: 0},
+            scratch_shapes=[pltpu.SemaphoreType.DMA((K, max(A, A * (B - 1))))],
+            compiler_params=pltpu.CompilerParams(**small),
+        )(written, tail)
         return (new_master, new_momentum, weights.reshape(total_rows, width))
 
     return jax.shard_map(

time: 149 us -> 144 us (0.966)
  Pallas kernels: 147 us -> 141 us
    pallas_call x2 -> x4, Pallas kernels: 147 us -> 141 us  [the longest x1 119 us: local(): pl.pallas_call(functools.partial(kernel, (A, B, F, K, sub, width, blocks,...]
where the time goes in v3:
time: 144 us; the launch traced here: 142 us
  Pallas kernels  141 us (98%)
    pallas_call x1, Pallas kernels, local(): pl.pallas_call(functools.partial(kernel, (A, B, F, K, sub, width, blocks,...  119 us
    pallas_call x1, Pallas kernels, local(): pl.pallas_call(functools.partial(gather_late, plan), out_shape=pltpu.VMEM...  15.5 us
    pallas_call x1, Pallas kernels, local(): pl.pallas_call(functools.partial(write_early, plan), out_shape=(jax.Shape...  5.69 us

profile of v3, /device:TPU:27, one launch (start us, length us, event | category | flops | bytes accessed | tf_op | source)
XLA Modules:
  0.0 142.0 jit_solution(13581395273525797520)
XLA Ops:
  0.6 118.6 %shard_map.67 = (f32[256,4096]{1,0:T(8,128)S(1)}, f32[256,4096]{1,0:T(8,128)S(1)}, bf16[32,16,16,512]{3,2,1,0:T(8,128)(2,1)S(1)}) custom-call(s32[32,16,16,512]{3,2,1,0:T(8,128)} %bitcast.2, f32[1,4,8192]{2,1,0:T(4,128)} %scales.1, f32[256,4096]{1,0:T(8,128)} %master.1, f32[256,4096]{1,0:T(8,128)} %momentum.1), custom_call_target="tpu_custom_call" | custom-call | tf_op jit(solution)/shard_map/pallas_call | solution.py:498
  119.3 5.7 %shard_map.68 = (f32[256,4096]{1,0:T(8,128)}, f32[256,4096]{1,0:T(8,128)}, bf16[32,16,16,512]{3,2,1,0:T(8,128)(2,1)}, f32[8,128]{1,0:T(8,128)S(1)}) custom-call(f32[256,4096]{1,0:T(8,128)S(1)} %get-tuple-element.10.master, f32[256,4096]{1,0:T(8,128)S(1)} %get-tuple-element.11.momentum, bf16[32,16,16,512]{3,2,1,0:T(8,128)(2,1)S(1)} %get-tuple-element.12.weights), custom_call_target="tpu_custom_call" | custom-call | tf_op jit(solution)/shard_map/pallas_call | solution.py:533
  124.9 15.5 %shard_map.69.tail = bf16[8,16,16,512]{3,2,1,0:T(8,128)(2,1)S(1)} custom-call(bf16[32,16,16,512]{3,2,1,0:T(8,128)(2,1)S(1)} %get-tuple-element.12.weights, f32[8,128]{1,0:T(8,128)S(1)} %get-tuple-element.16.token), custom_call_target="tpu_custom_call" | custom-call | tf_op jit(solution)/shard_map/pallas_call | solution.py:549
  140.4 1.6 %shard_map.70 = bf16[32,16,16,512]{3,2,1,0:T(8,128)(2,1)} custom-call(bf16[32,16,16,512]{3,2,1,0:T(8,128)(2,1)} %get-tuple-element.15.written, bf16[8,16,16,512]{3,2,1,0:T(8,128)(2,1)S(1)} %shard_map.69.tail), custom_call_target="tpu_custom_call", output_to_operand_aliasing={{}: (0, {})} | custom-call | tf_op jit(solution)/shard_map/pallas_call | solution.py:557

commit v4 on v3

--- a/solution.py
+++ b/solution.py
@@ -13,9 +13,9 @@
 momentum_factor = 0.9
 
 LAGS = (0, 3, 6, 8, 10, 13, 13, 16)
-EARLY = (8, 10, 16)
+EARLY = (10, 8, 16)
 LONG = 0
-TAIL = 10
+TAIL = 11
 RS1, RS2, X1, X2, AG1, AG2 = range(6)
 
 
@@ -57,13 +57,15 @@
         return lax.rem(f + 1 + i, F)
 
     barrier = pltpu.get_barrier_semaphore()
-    near = f - odd_core + 1
-    for i in range(A - 1):
-        pl.semaphore_signal(barrier, inc=1, device_id=(a_peer(i) * B + b, near), device_id_type=MESH)
-    for i in range(B - 1):
-        pl.semaphore_signal(barrier, inc=1, device_id=(a * B + b_peer(i), near), device_id_type=MESH)
-
-    @pl.when(odd_core == 0)
+    corner = R - 1
+    is_corner = r == corner
+    even_f = f - odd_core
+    near = [(a_peer(i) * B + b) for i in range(A - 1)] + [(a * B + b_peer(i)) for i in range(B - 1)]
+    for peer in near:
+        device = (peer, jnp.where(peer == corner, even_f + 1, f))
+        pl.semaphore_signal(barrier, inc=1, device_id=device, device_id_type=MESH)
+
+    @pl.when(is_corner & (odd_core == 0))
     def _():
         pl.semaphore_signal(barrier, inc=1, device_id=partner, device_id_type=MESH)
 
@@ -96,7 +98,11 @@
 
     for i in range(F // 2 - 1):
         pair = lax.rem(f // 2 + 1 + i, F // 2)
-        pl.semaphore_signal(barrier, inc=1, device_id=(r, 2 * pair), device_id_type=MESH)
+        pl.semaphore_signal(barrier, inc=1, device_id=(corner, 2 * pair), device_id_type=MESH)
+
+    @pl.when(jnp.logical_not(is_corner) | (odd_core == 1))
+    def _():
+        pl.semaphore_signal(barrier, inc=1, device_id=(corner, even_f), device_id_type=MESH)
 
     state_in = (
         pltpu.make_async_copy(master, new_master, state_sem.at[0]),
@@ -191,12 +197,16 @@
                 turn_scales(0, q)
             scale_piece(k, q)
             if n == 0:
-                @pl.when(odd_core == 1)
+                @pl.when(jnp.logical_not(is_corner))
+                def _():
+                    pl.semaphore_wait(barrier, A + B - 2)
+
+                @pl.when(is_corner & (odd_core == 1))
                 def _():
                     pl.semaphore_wait(barrier, 2 * (A + B - 2) + 1)
                     pl.semaphore_signal(near_sem, inc=1, device_id=partner, device_id_type=MESH)
 
-                @pl.when(odd_core == 0)
+                @pl.when(is_corner & (odd_core == 0))
                 def _():
                     pl.semaphore_wait(near_sem, 1)
 
@@ -269,12 +279,15 @@
 
         by_parity(k, go)
 
-        @pl.when((k == 0) & (odd_core == 0))
+        @pl.when((k == 0) & is_corner & (odd_core == 0))
         def _():
-            pl.semaphore_wait(barrier, F - 2)
+            pl.semaphore_wait(barrier, R * F - 1)
+            for q in range(R - 1):
+                for c in range(2):
+                    pl.semaphore_signal(far_sem, inc=1, device_id=(q, f + c), device_id_type=MESH)
             pl.semaphore_signal(far_sem, inc=1, device_id=partner, device_id_type=MESH)
 
-        @pl.when((k == 0) & (odd_core == 1))
+        @pl.when((k == 0) & (jnp.logical_not(is_corner) | (odd_core == 1)))
         def _():
             pl.semaphore_wait(far_sem, 1)
 

time: 144 us -> 143 us (level); the launches traced: 142 us -> 143 us
    pallas_call x1, Pallas kernels: 119 us -> 124 us  [local(): pl.pallas_call(functools.partial(kernel, (A, B, F, K, sub, width, blocks,...]
    pallas_call x1, Pallas kernels: 15.5 us -> 11.2 us  [local(): pl.pallas_call(functools.partial(gather_late, plan), out_shape=pltpu.VMEM...]
where the time goes in v4:
time: 143 us
  Pallas kernels  142 us (99%)
    pallas_call x1, Pallas kernels, local(): pl.pallas_call(functools.partial(kernel, (A, B, F, K, sub, width, blocks,...  124 us
    pallas_call x1, Pallas kernels, local(): pl.pallas_call(functools.partial(gather_late, plan), out_shape=pltpu.VMEM...  11.2 us
    pallas_call x1, Pallas kernels, local(): pl.pallas_call(functools.partial(write_early, plan), out_shape=(jax.Shape...  5.85 us

profile of v4, /device:TPU:27, one launch (start us, length us, event | category | flops | bytes accessed | tf_op | source)
XLA Modules:
  0.0 143.0 jit_solution(12196785253036220488)
XLA Ops:
  0.6 123.8 %shard_map.67 = (f32[256,4096]{1,0:T(8,128)S(1)}, f32[256,4096]{1,0:T(8,128)S(1)}, bf16[32,16,16,512]{3,2,1,0:T(8,128)(2,1)S(1)}) custom-call(s32[32,16,16,512]{3,2,1,0:T(8,128)} %bitcast.2, f32[1,4,8192]{2,1,0:T(4,128)} %scales.1, f32[256,4096]{1,0:T(8,128)} %master.1, f32[256,4096]{1,0:T(8,128)} %momentum.1), custom_call_target="tpu_custom_call" | custom-call | tf_op jit(solution)/shard_map/pallas_call | solution.py:511
  124.5 5.8 %shard_map.68 = (f32[256,4096]{1,0:T(8,128)}, f32[256,4096]{1,0:T(8,128)}, bf16[32,16,16,512]{3,2,1,0:T(8,128)(2,1)}, f32[8,128]{1,0:T(8,128)S(1)}) custom-call(f32[256,4096]{1,0:T(8,128)S(1)} %get-tuple-element.10.master, f32[256,4096]{1,0:T(8,128)S(1)} %get-tuple-element.11.momentum, bf16[32,16,16,512]{3,2,1,0:T(8,128)(2,1)S(1)} %get-tuple-element.12.weights), custom_call_target="tpu_custom_call" | custom-call | tf_op jit(solution)/shard_map/pallas_call | solution.py:546
  130.3 11.2 %shard_map.69.tail = bf16[6,16,16,512]{3,2,1,0:T(8,128)(2,1)S(1)} custom-call(bf16[32,16,16,512]{3,2,1,0:T(8,128)(2,1)S(1)} %get-tuple-element.12.weights, f32[8,128]{1,0:T(8,128)S(1)} %get-tuple-element.16.token), custom_call_target="tpu_custom_call" | custom-call | tf_op jit(solution)/shard_map/pallas_call | solution.py:562
  141.5 1.4 %shard_map.70 = bf16[32,16,16,512]{3,2,1,0:T(8,128)(2,1)} custom-call(bf16[32,16,16,512]{3,2,1,0:T(8,128)(2,1)} %get-tuple-element.15.written, bf16[6,16,16,512]{3,2,1,0:T(8,128)(2,1)S(1)} %shard_map.69.tail), custom_call_target="tpu_custom_call", output_to_operand_aliasing={{}: (0, {})} | custom-call | tf_op jit(solution)/shard_map/pallas_call | solution.py:570

commit v5 on v4

--- a/solution.py
+++ b/solution.py
@@ -89,12 +89,16 @@
         (k, p, ((1 + p % A) % A, (1 + p // A) % B) if k == 0 else ((1 + p // B) % A, (1 + p % B) % B))
         for p in range(R) for k in range(min(2, K))
     )
-    seen = set()
-    for k, p, spot in first:
-        if spot not in seen:
-            seen.add(spot)
-            scales_in(at(*spot)).start()
-        load(k, at(*spot)).start()
+    opening = min(2, K)
+
+    def fetch(pieces, seen):
+        for k, p, spot in pieces:
+            if spot not in seen:
+                seen.add(spot)
+                scales_in(at(*spot)).start()
+            load(k, at(*spot)).start()
+
+    fetch(first[:opening], set())
 
     for i in range(F // 2 - 1):
         pair = lax.rem(f // 2 + 1 + i, F // 2)
@@ -197,6 +201,8 @@
                 turn_scales(0, q)
             scale_piece(k, q)
             if n == 0:
+                fetch(first[opening:], {spot for _, _, spot in first[:opening]})
+
                 @pl.when(jnp.logical_not(is_corner))
                 def _():
                     pl.semaphore_wait(barrier, A + B - 2)

time: 143 us -> 143 us (level)
  no operation moved by 1% of the time
where the time goes in v5:
time: 143 us
  Pallas kernels  142 us (99%)
    pallas_call x1, Pallas kernels, local(): pl.pallas_call(functools.partial(kernel, (A, B, F, K, sub, width, blocks,...  124 us
    pallas_call x1, Pallas kernels, local(): pl.pallas_call(functools.partial(gather_late, plan), out_shape=pltpu.VMEM...  11.2 us
    pallas_call x1, Pallas kernels, local(): pl.pallas_call(functools.partial(write_early, plan), out_shape=(jax.Shape...  5.85 us

profile of v5, /device:TPU:27, one launch (start us, length us, event | category | flops | bytes accessed | tf_op | source)
XLA Modules:
  0.0 142.8 jit_solution(10314165691814011407)
XLA Ops:
  0.6 123.7 %shard_map.67 = (f32[256,4096]{1,0:T(8,128)S(1)}, f32[256,4096]{1,0:T(8,128)S(1)}, bf16[32,16,16,512]{3,2,1,0:T(8,128)(2,1)S(1)}) custom-call(s32[32,16,16,512]{3,2,1,0:T(8,128)} %bitcast.2, f32[1,4,8192]{2,1,0:T(4,128)} %scales.1, f32[256,4096]{1,0:T(8,128)} %master.1, f32[256,4096]{1,0:T(8,128)} %momentum.1), custom_call_target="tpu_custom_call" | custom-call | tf_op jit(solution)/shard_map/pallas_call | solution.py:517
  124.3 5.8 %shard_map.68 = (f32[256,4096]{1,0:T(8,128)}, f32[256,4096]{1,0:T(8,128)}, bf16[32,16,16,512]{3,2,1,0:T(8,128)(2,1)}, f32[8,128]{1,0:T(8,128)S(1)}) custom-call(f32[256,4096]{1,0:T(8,128)S(1)} %get-tuple-element.10.master, f32[256,4096]{1,0:T(8,128)S(1)} %get-tuple-element.11.momentum, bf16[32,16,16,512]{3,2,1,0:T(8,128)(2,1)S(1)} %get-tuple-element.12.weights), custom_call_target="tpu_custom_call" | custom-call | tf_op jit(solution)/shard_map/pallas_call | solution.py:552
  130.2 11.2 %shard_map.69.tail = bf16[6,16,16,512]{3,2,1,0:T(8,128)(2,1)S(1)} custom-call(bf16[32,16,16,512]{3,2,1,0:T(8,128)(2,1)S(1)} %get-tuple-element.12.weights, f32[8,128]{1,0:T(8,128)S(1)} %get-tuple-element.16.token), custom_call_target="tpu_custom_call" | custom-call | tf_op jit(solution)/shard_map/pallas_call | solution.py:568
  141.4 1.4 %shard_map.70 = bf16[32,16,16,512]{3,2,1,0:T(8,128)(2,1)} custom-call(bf16[32,16,16,512]{3,2,1,0:T(8,128)(2,1)} %get-tuple-element.15.written, bf16[6,16,16,512]{3,2,1,0:T(8,128)(2,1)S(1)} %shard_map.69.tail), custom_call_target="tpu_custom_call", output_to_operand_aliasing={{}: (0, {})} | custom-call | tf_op jit(solution)/shard_map/pallas_call | solution.py:576
